TPU v7x, 1024 devices: a whole 8x8x8 slice. The times are simulated.
1024 devices in a mesh: ctx: 32 (over z, x_hi, core), tp: 32 (over x_lo, y).
Axes of the slice: x: 8 (x_hi: 2, x_lo: 4; x = x_hi * 4 + x_lo), y: 8, z: 8, core: 2. Of those that a mesh axis runs over, the one named last changes fastest.
Arguments:
- act_codes: bfloat16 [8192, 4096], P(('ctx', 'tp')), may hold values from -24 to 24
- scale_exps: int32 [8192, 32], P(('ctx', 'tp')), may hold values from -2 to 2
- weight: bfloat16 [4096, 6144], P(None, 'tp'), may hold values from -0.09375 to 0.09375
- grad_out: bfloat16 [8192, 6144], P('ctx', 'tp'), may hold values from -6 to 6
Outputs:
- grad_input: bfloat16 [8192, 4096], P(('ctx', 'tp'))
- grad_weight: float32 [4096, 6144], P('ctx', 'tp')
All inputs are finite; a program needn't handle non-finite values.
Results may differ from a plain program's by a relative error of at most 0.023.
Values may be sent and summed in bfloat16 or wider, within the bound.
A program may use at most 32 MiB of HBM per device.

v0:
```python
import jax
import jax.numpy as jnp
from jax import lax
from jax.sharding import PartitionSpec as P


def copy_for_each(array, axis):
    copies = jnp.broadcast_to(array, (lax.axis_size(axis), *array.shape))
    return lax.all_to_all(copies, axis, split_axis=0, concat_axis=0, tiled=True)


def in_order(tiles, dim):
    tiles = jnp.moveaxis(tiles, 0, dim)
    shape = tiles.shape
    return tiles.reshape(*shape[:dim], shape[dim] * shape[dim + 1], *shape[dim + 2 :])


def gather_directly(array, axis, dim):
    tiles = copy_for_each(array, axis)
    return in_order(tiles, dim)


def split_up(array, dim, size):
    shape = array.shape
    tiles = array.reshape(*shape[:dim], size, shape[dim] // size, *shape[dim + 1 :])
    return jnp.moveaxis(tiles, dim, 0)


def sum_at_owner(array, axis, dim):
    tiles = split_up(array, dim, lax.axis_size(axis))
    arrived = lax.all_to_all(tiles, axis, split_axis=0, concat_axis=0, tiled=True)
    return arrived.astype(jnp.float32).sum(axis=0)


def dequantize(codes, exponents, block):
    tok_rows, width = codes.shape
    scales = jnp.exp2(exponents.astype(jnp.float32))
    blocked = (
        codes.astype(jnp.float32).reshape(tok_rows, width // block, block) * scales[:, :, None]
    )
    return blocked.reshape(tok_rows, width).astype(jnp.bfloat16)


def body(act_codes, scale_exps, weight, grad_out):
    width = act_codes.shape[1]
    block = width // scale_exps.shape[1]
    acts = dequantize(act_codes, scale_exps, block)
    add_acts = gather_directly(acts, "tp", 0)
    grads = grad_out
    partial_sum = lax.dot_general(
        add_acts, grads, (((0,), (0,)), ((), ())), preferred_element_type=jnp.float32
    )
    summed = lax.psum_scatter(
        partial_sum.astype(jnp.bfloat16), "ctx", scatter_dimension=0, tiled=True
    ).astype(jnp.float32)
    tokens_all = grad_out.shape[0] * lax.axis_size("ctx")
    grad_weight = summed * lax.rsqrt(jnp.float32(tokens_all))
    grads = grad_out
    grad_input = sum_at_owner(
        lax.dot_general(
            grads, weight, (((1,), (1,)), ((), ())), preferred_element_type=jnp.float32
        ).astype(jnp.bfloat16),
        "tp",
        0,
    ).astype(jnp.bfloat16)
    return (grad_input, grad_weight)


def solution(mesh):
    placed = (P(("ctx", "tp"), None), P(("ctx", "tp"), None), P(None, "tp"), P("ctx", "tp"))
    return jax.shard_map(
        body,
        mesh=mesh,
        in_specs=placed,
        out_specs=(P(("ctx", "tp"), None), P("ctx", "tp")),
        check_vma=False,
    )
```

profile of v0, /device:TPU:1, one launch (start us, length us, event | category | flops | bytes accessed | tf_op | source)
XLA Modules:
  0.0 256.9 jit_solution(497369837242557830)
XLA Ops:
  7.2 0.0 copy-start
  7.2 0.8 multiply_exponential_fusion
  8.0 0.1 copy.7
  8.1 0.9 fusion.2
  9.0 1.5 broadcast_in_dim.4
  10.6 0.0 copy-start.1
  10.6 11.5 %all-to-all-start.1 = ((bf16[32,8,4096]{2,1,0:T(8,128)(2,1)}), bf16[32,8,4096]{2,1,0:T(8,128)(2,1)}, u32[]{:S(2)}, u32[]{:S(2)}) async-start(bf16[32,8,4096]{2,1,0:T(8,128)(2,1)} %broadcast_in_dim.4), calls=%async_computation.1 | async-start | bytes 4194304 | tf_op jit(solution)/shard_map/all_to_all | solution.py:9
  22.1 0.0 copy-done
  22.1 0.0 copy-done.1
  22.1 2.1 fusion
  24.2 53.5 %all-to-all-done.1 = bf16[32,8,4096]{2,1,0:T(8,128)(2,1)} async-done(((bf16[32,8,4096]{2,1,0:T(8,128)(2,1)}), bf16[32,8,4096]{2,1,0:T(8,128)(2,1)}, u32[]{:S(2)}, u32[]{:S(2)}) %all-to-all-start.1) | async-done | bytes 2097184 | tf_op jit(solution)/shard_map/all_to_all | solution.py:9
  77.7 5.5 %all-to-all-start = ((bf16[32,8,4096]{2,1,0:T(8,128)(2,1)}), bf16[32,8,4096]{2,1,0:T(8,128)(2,1)}, u32[]{:S(2)}, u32[]{:S(2)}) async-start(bf16[32,8,4096]{2,1,0:T(8,128)(2,1)} %fusion), calls=%async_computation | async-start | bytes 4194304 | tf_op jit(solution)/shard_map/all_to_all | solution.py:31
  83.2 0.0 reduce-scatter.4.cloned.1.call-start
  83.3 2.2 convolution_convert_fusion.1
  85.5 2.5 copy.8
  87.9 0.0 reduce-scatter.4.cloned.1.call-update
  87.9 49.7 %all-to-all-done = bf16[32,8,4096]{2,1,0:T(8,128)(2,1)} async-done(((bf16[32,8,4096]{2,1,0:T(8,128)(2,1)}), bf16[32,8,4096]{2,1,0:T(8,128)(2,1)}, u32[]{:S(2)}, u32[]{:S(2)}) %all-to-all-start) | async-done | bytes 2097184 | tf_op jit(solution)/shard_map/all_to_all | solution.py:31
  137.6 2.6 reduce_sum.12
  140.2 108.2 %reduce-scatter.4.cloned.1.call-done = bf16[128,192]{1,0:T(8,128)(2,1)} async-done(((bf16[4096,192]{1,0:T(8,128)(2,1)}), bf16[128,192]{1,0:T(8,128)(2,1)}) %reduce-scatter.4.cloned.1.call-update) | async-done | bytes 49168
  248.4 0.9 copy.9
  249.4 0.7 convert_multiply_fusion
Async XLA Ops:
  7.2 14.9 %copy-start = (bf16[4096,192]{0,1:T(8,128)(2,1)S(1)}, bf16[4096,192]{0,1:T(8,128)(2,1)}, u32[]{:S(2)}) copy-start(bf16[4096,192]{0,1:T(8,128)(2,1)} %param.6) | copy-start | bytes 4718596
  10.6 11.5 %copy-start.1 = (bf16[256,192]{0,1:T(8,128)(2,1)S(1)}, bf16[256,192]{0,1:T(8,128)(2,1)}, u32[]{:S(2)}) copy-start(bf16[256,192]{0,1:T(8,128)(2,1)} %param.7) | copy-start | bytes 294916
  10.6 67.1 %all-to-all-start.1 = ((bf16[32,8,4096]{2,1,0:T(8,128)(2,1)}), bf16[32,8,4096]{2,1,0:T(8,128)(2,1)}, u32[]{:S(2)}, u32[]{:S(2)}) async-start(bf16[32,8,4096]{2,1,0:T(8,128)(2,1)} %broadcast_in_dim.4), calls=%async_computation.1 | async-start | bytes 4194304 | tf_op jit(solution)/shard_map/all_to_all | solution.py:9
  77.7 59.9 %all-to-all-start = ((bf16[32,8,4096]{2,1,0:T(8,128)(2,1)}), bf16[32,8,4096]{2,1,0:T(8,128)(2,1)}, u32[]{:S(2)}, u32[]{:S(2)}) async-start(bf16[32,8,4096]{2,1,0:T(8,128)(2,1)} %fusion), calls=%async_computation | async-start | bytes 4194304 | tf_op jit(solution)/shard_map/all_to_all | solution.py:31
  83.2 165.2 %reduce-scatter.4.cloned.1.call-start = ((), (), s32[]{:S(2)}) async-start(), calls=%async_computation.3 | async-start | bytes 2162688
Sparse Core Ops, SparseCore 0:
  89.9 158.4 reduce-scatter.3
where the time goes:
time: 261 us; the launch traced here: 257 us
  waiting for transfers between devices  211 us (81%)
  starting transfers between devices  17.1 us (7%)
  between operations  14.1 us (5%)
  local copies, waits for them, and re-layouts  5.03 us (2%)
  other arithmetic  4.97 us (2%)
  matrix products  4.24 us (2%)
    unnamed x2, waiting for transfers between devices  108 us
    all_to_all x1, waiting for transfers between devices, copy_for_each(): return lax.all_to_all(copies, axis, split_axis=0, concat_axis=0, tiled=True)  53.5 us
    all_to_all x1, waiting for transfers between devices, sum_at_owner(): lax.all_to_all(tiles, axis, split_axis=0, concat_axis=0, tiled=True)  49.7 us
    all_to_all x1, starting transfers between devices, copy_for_each(): return lax.all_to_all(copies, axis, split_axis=0, concat_axis=0, tiled=True)  11.5 us
    all_to_all x1, starting transfers between devices, sum_at_owner(): lax.all_to_all(tiles, axis, split_axis=0, concat_axis=0, tiled=True)  5.53 us
  transfers between devices with their start and end apart: 3, of which 3 were waited for; matrix products, arithmetic and copies ran while one was open for 4% of the time, Pallas kernels for 0%

commit v1 on v0

v1 whole, which is shorter than its diff:
```python
import functools

import jax
import jax.numpy as jnp
from jax import lax
from jax.experimental import pallas as pl
from jax.experimental.pallas import tpu as pltpu
from jax.sharding import PartitionSpec as P

DIMS = {"z": 8, "xh": 2, "core": 2, "xl": 4, "y": 8}
GROUPS = 4


def ring_pieces(half, groups):
    low, high = tuple(range(groups // 2)), tuple(range(groups // 2, groups))
    ways = []
    for first, rest in ((low, high), (high, low)):
        order = [(1, g) for g in first]
        for step in range(2, half + 1):
            order += [(step, g) for g in rest + first]
        ways.append(order)
    return ways


def kernel(
    dims, scale, codes_hbm, exps_hbm, w_hbm, g_hbm, gi_ref, gw_ref,
    codes, exps, w, g, in_sem,
    s_buf, a1, ab, at, gp, ga, rest, parts, rb, xs, xr, own,
    dwf, dwb, rz, fs, fr,
    s_send, s_recv, a_send, a_recv, g_send, g_recv, p_send, p_recv,
    z_send, z_recv, x_send, x_recv, f_send, f_recv,
):
    nz, nh, nc, nx, ny = dims["z"], dims["xh"], dims["core"], dims["xl"], dims["y"]
    hy, hz = ny // 2, nz // 2
    f32, bf16 = jnp.float32, jnp.bfloat16
    ctx, tp = lax.axis_index("ctx"), lax.axis_index("tp")
    z, xh, c = ctx // (nh * nc), (ctx // nc) % nh, ctx % nc
    xl, y = tp // ny, tp % ny

    def at_z(d):
        return {"ctx": ((z + d + nz) % nz * nh + xh) * nc + c, "tp": tp}

    def at_y(d):
        return {"ctx": ctx, "tp": xl * ny + (y + d + ny) % ny}

    def at_x(dx, dc=0, dh=0):
        return {
            "ctx": (z * nh + (xh + dh) % nh) * nc + (c + dc) % nc,
            "tp": (xl + dx) % nx * ny + y,
        }

    rows, width = codes.shape
    toks, cols = g.shape
    blocks = exps.shape[1]
    quarter = 128 // nx
    feats = width // (nc * nx)
    per = rows * nx
    glanes = width // GROUPS
    sent = []

    def send(src, dst, ssem, rsem, dev):
        copy = pltpu.make_async_remote_copy(
            src_ref=src, dst_ref=dst, send_sem=ssem, recv_sem=rsem,
            device_id=dev, device_id_type=pl.DeviceIdType.MESH,
        )
        copy.start()
        sent.append(copy)
        return copy

    loads = []
    for i, (src, dst) in enumerate(((codes_hbm, codes), (exps_hbm, exps), (g_hbm, g), (w_hbm, w))):
        copy = pltpu.make_async_copy(src, dst, in_sem.at[i])
        copy.start()
        loads.append(copy)

    barrier = pltpu.get_barrier_semaphore()
    mates = [(dx, dc) for dx in range(nx) for dc in range(nc) if (dx, dc) != (0, 0)]
    finals = [(dh, dx) for dh in range(nh) for dx in range(nx) if (dh, dx) != (0, 0)]
    peers = [at_x(dx, dc) for dx, dc in mates]
    peers += [at_x(dx, 0, dh) for dh, dx in finals if dh != 0]
    peers += [at_y(1), at_y(-1), at_z(1), at_z(-1)]
    for dev in peers:
        pl.semaphore_signal(barrier, inc=1, device_id=dev, device_id_type=pl.DeviceIdType.MESH)

    loads[0].wait()
    loads[1].wait()
    scales = jnp.exp2(exps[...].astype(f32))
    lane = lax.broadcasted_iota(jnp.int32, (rows, 128), 1) // quarter
    acts = [
        codes[:, b * 128 : (b + 1) * 128].astype(f32) * scales[:, b : b + 1] for b in range(blocks)
    ]
    for xi in range(nx):
        for ci in range(nc):
            mine = [acts[b] for b in range(blocks) if b % nc == ci]
            for m in range(len(mine) // nx):
                out = mine[m * nx]
                if xi:
                    out = pltpu.roll(out, (128 - xi * quarter) % 128, 1)
                for i in range(1, nx):
                    piece, shift = mine[m * nx + i], ((i - xi) * quarter) % 128
                    if shift:
                        piece = pltpu.roll(piece, shift, 1)
                    out = jnp.where(lane == i, piece, out)
                s_buf[xi * nc + ci, :, m * 128 : (m + 1) * 128] = out.astype(bf16)
    a1[xl * nc + c] = s_buf[xl * nc + c]

    loads[2].wait()
    raw = g[...].astype(f32)
    raw = jnp.concatenate(
        [
            raw[(i * ny + j) * rows : (i * ny + j + 1) * rows]
            for j in range(ny) for i in range(nx)
        ],
        axis=0,
    )
    gp[...] = raw.astype(bf16)
    ga[c, xl, :toks, :] = raw[:, :128].astype(bf16)
    tail = raw[:, 128:]
    ga[c, xl, toks:, :] = jnp.concatenate([tail[: toks // 2], tail[toks // 2 :]], axis=1).astype(bf16)

    pl.semaphore_wait(barrier, len(peers))

    s_wait = []
    for k, (dx, dc) in enumerate(mates):
        s_wait.append(
            send(
                s_buf.at[(xl + dx) % nx * nc + (c + dc) % nc], a1.at[xl * nc + c],
                s_send.at[k], s_recv.at[k], at_x(dx, dc),
            )
        )
    g_wait = []
    for dx in range(1, nx):
        g_wait.append(
            send(ga.at[c, xl], ga.at[c, xl], g_send.at[dx - 1], g_recv.at[dx - 1], at_x(dx))
        )
    twin_wait = [
        send(ga.at[c, xl], ga.at[c, xl], g_send.at[nx - 1], g_recv.at[nx - 1], at_x(0, 1))
    ]

    loads[3].wait()
    step_w = min(width, 512)
    for n in range(width // step_w):
        part = lax.dot_general(
            gp[...], w[n * step_w : (n + 1) * step_w, :], (((1,), (1,)), ((), ())),
            preferred_element_type=f32,
        )
        parts[:, :, n * step_w : (n + 1) * step_w] = part.astype(bf16).reshape(ny, per, step_w)

    p_orders = ring_pieces(hy, GROUPS)
    p_index = [{piece: i for i, piece in enumerate(order)} for order in p_orders]
    p_copies = [{}, {}]
    p_next = [0, 0]

    def p_piece(way):
        if p_next[way] >= len(p_orders[way]):
            return
        step, grp = p_orders[way][p_next[way]]
        p_next[way] += 1
        sign = 1 - 2 * way
        off = hy + 1 - step
        lanes = slice(grp * glanes, (grp + 1) * glanes)
        dest = (y + sign * off + ny) % ny
        if (step - 1, grp) in p_copies[way]:
            p_copies[way][(step - 1, grp)].wait_recv()
            total = rb[way, step - 2, :, lanes].astype(f32) + parts[dest, :, lanes].astype(f32)
            rb[way, step - 2, :, lanes] = total.astype(bf16)
            src = rb.at[way, step - 2, :, lanes]
        else:
            src = parts.at[dest, :, lanes]
        i = p_index[way][(step, grp)]
        p_copies[way][(step, grp)] = send(
            src, rb.at[way, step - 1, :, lanes], p_send.at[way, i], p_recv.at[way, i], at_y(sign)
        )

    def p_both(count=1):
        for _ in range(count):
            p_piece(0)
            p_piece(1)

    p_both(GROUPS // 2)

    for copy in s_wait:
        copy.wait_recv()
    for ci in range(nc):
        ab[y, ci] = jnp.concatenate(
            [a1[xi * nc + ci].astype(f32) for xi in range(nx)], axis=0
        ).astype(bf16)

    a_copies = [{}, {}]

    def a_piece(way, step, ci):
        sign = 1 - 2 * way
        if step > 1:
            a_copies[way][(step - 1, ci)].wait_recv()
        ref = ab.at[(y - sign * (step - 1) + ny) % ny, ci]
        i = (step - 1) * nc + ci
        a_copies[way][(step, ci)] = send(ref, ref, a_send.at[way, i], a_recv.at[way, i], at_y(sign))

    for step in range(1, hy + 1):
        for ci in range(nc):
            for way in (0, 1):
                if step < hy or ci % 2 == way:
                    a_piece(way, step, ci)
        p_both()

    for dx in range(1, nx):
        g_wait[dx - 1].wait_recv()
        ref = ga.at[c, (xl - dx + nx) % nx]
        twin_wait.append(
            send(ref, ref, g_send.at[nx - 1 + dx], g_recv.at[nx - 1 + dx], at_x(0, 1))
        )

    for way in (0, 1):
        for ci in range(nc):
            if (hy, ci) in a_copies[way]:
                a_copies[way][(hy, ci)].wait_recv()
            if hy > 1 and not (hy, ci) in a_copies[way]:
                a_copies[way][(hy - 1, ci)].wait_recv()
    for ci in range(nc):
        at[:, ci * toks : (ci + 1) * toks] = ab[:, ci].reshape(toks, feats).T
    for copy in twin_wait:
        copy.wait_recv()

    mains = nx * 128
    for ci in range(nc):
        for k in range(nx // 2):
            left = ga[ci, 2 * k, toks:, :].astype(f32)
            right = ga[ci, 2 * k + 1, toks:, :].astype(f32)
            first = lax.broadcasted_iota(jnp.int32, left.shape, 1) < 64
            top = jnp.where(first, left, pltpu.roll(right, 64, 1))
            bottom = jnp.where(first, pltpu.roll(left, 64, 1), right)
            lanes = slice(k * 128, (k + 1) * 128)
            rest[ci * toks : ci * toks + toks // 2, lanes] = top.astype(bf16)
            rest[ci * toks + toks // 2 : (ci + 1) * toks, lanes] = bottom.astype(bf16)
    zrows = feats // nz

    def dw_store(lanes, value):
        value = value.reshape(nz, zrows, value.shape[1])
        dwf[:, :, lanes] = value
        dwb[:, :, lanes] = value.astype(bf16)

    for k in range(nx // 2):
        total = None
        for ci in range(nc):
            both = jnp.concatenate([ga[ci, 2 * k, :toks, :], ga[ci, 2 * k + 1, :toks, :]], axis=1)
            part = jnp.dot(at[:, ci * toks : (ci + 1) * toks], both, preferred_element_type=f32)
            total = part if total is None else total + part
        dw_store(slice(k * 256, (k + 1) * 256), total)
    dw_store(slice(mains, mains + 64 * nx), jnp.dot(at[...], rest[...], preferred_element_type=f32))

    z_orders = ring_pieces(hz, 2)
    z_copies = [{}, {}]
    half_rows = zrows // 2

    def z_total(way, step, grp, dest):
        z_copies[way][(step, grp)].wait_recv()
        sub = slice(grp * half_rows, (grp + 1) * half_rows)
        return rz[way, step - 1, sub, :].astype(f32)

    def z_piece(way, i):
        step, grp = z_orders[way][i]
        sign = 1 - 2 * way
        dest = (z + sign * (hz + 1 - step) + nz) % nz
        sub = slice(grp * half_rows, (grp + 1) * half_rows)
        if (step - 1, grp) in z_copies[way]:
            total = z_total(way, step - 1, grp, dest) + dwf[dest, sub, :]
            rz[way, step - 2, sub, :] = total.astype(bf16)
            src = rz.at[way, step - 2, sub, :]
        else:
            src = dwb.at[dest, sub, :]
        z_copies[way][(step, grp)] = send(
            src, rz.at[way, step - 1, sub, :], z_send.at[way, i], z_recv.at[way, i], at_z(sign)
        )

    for i in range(len(z_orders[0])):
        z_piece(0, i)
        z_piece(1, i)
        p_both()

    f_wait = []
    sums = []
    for grp in range(2):
        sub = slice(grp * half_rows, (grp + 1) * half_rows)
        total = dwf[z, sub, :]
        for way in (0, 1):
            if (hz, grp) in z_copies[way]:
                total = total + z_total(way, hz, grp, z)
        sums.append(total)
    frows = zrows // nh
    total = sums if nh == 2 else [jnp.concatenate(sums, axis=0)]
    for hi in range(nh):
        for xi in range(nx):
            fs[hi, xi, :, :128] = total[hi][:, xi * 128 : (xi + 1) * 128].astype(bf16)
            lo = mains + xi // 2 * 128
            fs[hi, xi, :, 128:] = total[hi][:, lo : lo + 128].astype(bf16)
    fr[xh, xl] = fs[xh, xl]
    for k, (dh, dx) in enumerate(finals):
        f_wait.append(
            send(
                fs.at[(xh + dh) % nh, (xl + dx) % nx], fr.at[xh, xl],
                f_send.at[k], f_recv.at[k], at_x(dx, 0, dh),
            )
        )

    p_both(len(p_orders[0]))
    x_wait = {}
    for grp in p_orders_last(p_orders):
        lanes = slice(grp * glanes, (grp + 1) * glanes)
        total = parts[y, :, lanes].astype(f32)
        for way in (0, 1):
            if (hy, grp) in p_copies[way]:
                p_copies[way][(hy, grp)].wait_recv()
                total = total + rb[way, hy - 1, :, lanes].astype(f32)
        for xi in range(nx):
            piece = total[xi * rows : (xi + 1) * rows]
            own[xi, :, lanes] = piece
            xs[xi, :, lanes] = piece.astype(bf16)
        for dx in range(1, nx):
            x_wait[(grp, dx)] = send(
                xs.at[(xl + dx) % nx, :, lanes], xr.at[dx - 1, :, lanes],
                x_send.at[grp, dx - 1], x_recv.at[grp, dx - 1], at_x(dx),
            )

    for copy in f_wait:
        copy.wait_recv()
    odd = xl % 2 == 1
    for xi in range(nx):
        total = fr[0, xi].astype(f32)
        for hi in range(1, nh):
            total = total + fr[hi, xi].astype(f32)
        total = total * scale
        last = total[:, 128:]
        last = jnp.where(odd, pltpu.roll(last, 64, 1), last)
        gw_ref[xi * frows : (xi + 1) * frows, :128] = total[:, :128]
        gw_ref[xi * frows : (xi + 1) * frows, 128:] = last[:, :64]

    for grp in p_orders_last(p_orders):
        lanes = slice(grp * glanes, (grp + 1) * glanes)
        total = own[xl, :, lanes]
        for dx in range(1, nx):
            x_wait[(grp, dx)].wait_recv()
            total = total + xr[dx - 1, :, lanes].astype(f32)
        gi_ref[:, lanes] = total.astype(bf16)

    for copy in sent:
        copy.wait_send()


def p_orders_last(orders):
    last = orders[0][-1][0]
    return [g for s, g in orders[0] if s == last] if last > 1 else list(range(GROUPS))


def body(dims, act_codes, scale_exps, weight, grad_out):
    nz, nh, nc, nx, ny = dims["z"], dims["xh"], dims["core"], dims["xl"], dims["y"]
    hy, hz = ny // 2, nz // 2
    rows, width = act_codes.shape
    toks, cols = grad_out.shape
    out_rows = width // (nz * nh * nc)
    feats = width // (nc * nx)
    per = rows * nx
    dcols = nx * cols
    scale = float(1.0 / (toks * nz * nh * nc) ** 0.5)
    bf16, f32 = jnp.bfloat16, jnp.float32
    n_p = GROUPS // 2 + (hy - 1) * GROUPS
    n_z = 1 + (hz - 1) * 2

    def vm(shape, kind=bf16):
        return pltpu.VMEM(shape, kind)

    def sems(*shape):
        return pltpu.SemaphoreType.DMA(shape)

    scratch = [
        vm(act_codes.shape), vm(scale_exps.shape, jnp.int32), vm(weight.shape), vm(grad_out.shape),
        sems(4),
        vm((nx * nc, rows, feats)), vm((nx * nc, rows, feats)), vm((ny, nc, per, feats)),
        vm((feats, nc * toks)), vm((toks, cols)), vm((nc, nx, toks * 3 // 2, 128)),
        vm((nc * toks, 64 * nx)), vm((ny, per, width)), vm((2, hy, per, width)),
        vm((nx, rows, width)), vm((nx - 1, rows, width)), vm((nx, rows, width), f32),
        vm((nz, feats // nz, dcols), f32), vm((nz, feats // nz, dcols)),
        vm((2, hz, feats // nz, dcols)),
        vm((nh, nx, out_rows // nx, 256)), vm((nh, nx, out_rows // nx, 256)),
        sems(nx * nc - 1), sems(nx * nc - 1),
        sems(2, hy * nc), sems(2, hy * nc),
        sems(2 * nx - 1), sems(2 * nx - 1),
        sems(2, n_p), sems(2, n_p),
        sems(2, n_z), sems(2, n_z),
        sems(GROUPS, nx - 1), sems(GROUPS, nx - 1),
        sems(nh * nx - 1), sems(nh * nx - 1),
    ]
    return pl.pallas_call(
        functools.partial(kernel, dims, scale),
        out_shape=(
            jax.ShapeDtypeStruct((rows, width), bf16),
            jax.ShapeDtypeStruct((out_rows, cols), f32),
        ),
        in_specs=[pl.BlockSpec(memory_space=pl.ANY)] * 4,
        out_specs=[pl.BlockSpec(memory_space=pltpu.VMEM)] * 2,
        scratch_shapes=scratch,
        compiler_params=pltpu.CompilerParams(
            collective_id=0, has_side_effects=True, vmem_limit_bytes=48 * 1024 * 1024
        ),
        name="backward",
    )(act_codes, scale_exps, weight, grad_out)


def solution(mesh):
    placed = (P(("ctx", "tp"), None), P(("ctx", "tp"), None), P(None, "tp"), P("ctx", "tp"))
    return jax.shard_map(
        functools.partial(body, DIMS),
        mesh=mesh,
        in_specs=placed,
        out_specs=(P(("ctx", "tp"), None), P("ctx", "tp")),
        check_vma=False,
    )
```

time: 261 us -> 70.8 us (0.27)
  the two profiles are of different devices: /device:TPU:1 before, /device:TPU:14 now
where the time goes in v1:
time: 70.8 us; the launch traced here: 70.6 us
  Pallas kernels  64.3 us (91%)
  local copies, waits for them, and re-layouts  5.56 us (8%)
    pallas_call x1, Pallas kernels, body(): pl.pallas_call(functools.partial(kernel, dims, scale), out_shape=(jax.Sha...  64.3 us
    unnamed x7, local copies, waits for them, and re-layouts  4.82 us

profile of v1, /device:TPU:14, one launch (start us, length us, event | category | flops | bytes accessed | tf_op | source)
XLA Modules:
  0.0 70.6 jit_solution(14551536140095392541)
XLA Ops:
  0.6 0.0 copy-start.1
  0.6 0.0 copy-start
  0.6 1.0 %copy.7.g_hbm = bf16[256,192]{1,0:T(8,128)(2,1)S(1)} copy(bf16[256,192]{0,1:T(8,128)(2,1)} %param.7) | data formatting | bytes 196608 | tf_op args[3]
  1.7 3.2 %copy.6.w_hbm = bf16[4096,192]{1,0:T(8,128)(2,1)S(1)} copy(bf16[4096,192]{0,1:T(8,128)(2,1)} %param.6) | data formatting | bytes 3145728 | tf_op args[2]
  4.8 0.0 copy-done.1
  4.9 0.0 copy-done
  4.9 64.3 %backward.1 = (bf16[8,4096]{1,0:T(8,128)(2,1)S(1)}, f32[128,192]{1,0:T(8,128)S(1)}) custom-call(bf16[8,4096]{1,0:T(8,128)(2,1)S(1)} %copy-done, s32[8,32]{1,0:T(8,128)S(1)} %copy-done.1, bf16[4096,192]{1,0:T(8,128)(2,1)S(1)} %copy.6.w_hbm, bf16[256,192]{1,0:T(8,128)(2,1)S(1)} %copy.7.g_hbm), custom_call_target="tpu_custom_call" | custom-call | tf_op jit(solution)/shard_map/backward/pallas_call | solution.py:392
  69.2 0.7 %copy.8 = f32[128,192]{0,1:T(8,128)} copy(f32[128,192]{1,0:T(8,128)S(1)} %get-tuple-element.3) | data formatting | bytes 196608 | tf_op jit(solution)/shard_map/backward/pallas_call | solution.py:392
  69.9 0.6 copy.10
Async XLA Ops:
  0.6 4.2 %copy-start.1 = (s32[8,32]{1,0:T(8,128)S(1)}, s32[8,32]{1,0:T(8,128)}, u32[]{:S(2)}) copy-start(s32[8,32]{1,0:T(8,128)} %exps_hbm.1) | copy-start | bytes 3076
  0.6 4.2 %copy-start = (bf16[8,4096]{1,0:T(8,128)(2,1)S(1)}, bf16[8,4096]{1,0:T(8,128)(2,1)}, u32[]{:S(2)}) copy-start(bf16[8,4096]{1,0:T(8,128)(2,1)} %codes_hbm.1) | copy-start | bytes 196612

commit v2 on v1

--- a/solution.py
+++ b/solution.py
@@ -8,7 +8,9 @@
 from jax.sharding import PartitionSpec as P
 
 DIMS = {"z": 8, "xh": 2, "core": 2, "xl": 4, "y": 8}
-GROUPS = 4
+GROUPS = 6
+Z_GROUPS = 4
+AFTER_AG1, AFTER_AG2, AFTER_Z1, AFTER_Z2 = 3, 3, 4, 5
 
 
 def ring_pieces(half, groups):
@@ -24,11 +26,12 @@
 
 def kernel(
     dims, scale, codes_hbm, exps_hbm, w_hbm, g_hbm, gi_ref, gw_ref,
-    codes, exps, w, g, in_sem,
+    codes, exps, w, wq, wr, g, in_sem,
     s_buf, a1, ab, at, gp, ga, rest, parts, rb, xs, xr, own,
-    dwf, dwb, rz, fs, fr,
+    dwf, dwb, rz, fs, fr, qp, rq, qs, qr,
     s_send, s_recv, a_send, a_recv, g_send, g_recv, p_send, p_recv,
     z_send, z_recv, x_send, x_recv, f_send, f_recv,
+    w_send, w_recv, q_send, q_recv, o_send, o_recv,
 ):
     nz, nh, nc, nx, ny = dims["z"], dims["xh"], dims["core"], dims["xl"], dims["y"]
     hy, hz = ny // 2, nz // 2
@@ -50,12 +53,13 @@
         }
 
     rows, width = codes.shape
-    toks, cols = g.shape
+    cols, toks = g.shape
     blocks = exps.shape[1]
     quarter = 128 // nx
     feats = width // (nc * nx)
     per = rows * nx
-    glanes = width // GROUPS
+    plain = width - 128 * nc * nx
+    glanes = plain // GROUPS
     sent = []
 
     def send(src, dst, ssem, rsem, dev):
@@ -68,7 +72,11 @@
         return copy
 
     loads = []
-    for i, (src, dst) in enumerate(((codes_hbm, codes), (exps_hbm, exps), (g_hbm, g), (w_hbm, w))):
+    moves = [(codes_hbm, codes), (exps_hbm, exps), (g_hbm, g), (w_hbm.at[:, :plain], w)]
+    for dx in range(nx):
+        first = pl.multiple_of(plain + ((xl + dx) % nx * nc + c) * 128, 128)
+        moves.append((w_hbm.at[:, pl.ds(first, 128)], wq.at[dx - 1] if dx else wr.at[xl]))
+    for i, (src, dst) in enumerate(moves):
         copy = pltpu.make_async_copy(src, dst, in_sem.at[i])
         copy.start()
         loads.append(copy)
@@ -78,7 +86,8 @@
     finals = [(dh, dx) for dh in range(nh) for dx in range(nx) if (dh, dx) != (0, 0)]
     peers = [at_x(dx, dc) for dx, dc in mates]
     peers += [at_x(dx, 0, dh) for dh, dx in finals if dh != 0]
-    peers += [at_y(1), at_y(-1), at_z(1), at_z(-1)]
+    peers += [at_y(d) for d in range(1, ny)]
+    peers += [at_z(d) for d in sorted({1, nz - 1, 2 % nz, (nz - 2) % nz} - {0})]
     for dev in peers:
         pl.semaphore_signal(barrier, inc=1, device_id=dev, device_id_type=pl.DeviceIdType.MESH)
 
@@ -105,7 +114,7 @@
     a1[xl * nc + c] = s_buf[xl * nc + c]
 
     loads[2].wait()
-    raw = g[...].astype(f32)
+    raw = g[...].astype(f32).T
     raw = jnp.concatenate(
         [
             raw[(i * ny + j) * rows : (i * ny + j + 1) * rows]
@@ -137,11 +146,19 @@
         send(ga.at[c, xl], ga.at[c, xl], g_send.at[nx - 1], g_recv.at[nx - 1], at_x(0, 1))
     ]
 
+    w_wait = []
+    for dx in range(nx):
+        loads[4 + dx].wait()
+        if dx:
+            w_wait.append(
+                send(wq.at[dx - 1], wr.at[xl], w_send.at[dx - 1], w_recv.at[dx - 1], at_x(dx))
+            )
+
     loads[3].wait()
-    step_w = min(width, 512)
-    for n in range(width // step_w):
+    step_w = min(plain, 512)
+    for n in range(plain // step_w):
         part = lax.dot_general(
-            gp[...], w[n * step_w : (n + 1) * step_w, :], (((1,), (1,)), ((), ())),
+            gp[...], w[:, n * step_w : (n + 1) * step_w], (((1,), (0,)), ((), ())),
             preferred_element_type=f32,
         )
         parts[:, :, n * step_w : (n + 1) * step_w] = part.astype(bf16).reshape(ny, per, step_w)
@@ -177,7 +194,7 @@
             p_piece(0)
             p_piece(1)
 
-    p_both(GROUPS // 2)
+    p_both(GROUPS)
 
     for copy in s_wait:
         copy.wait_recv()
@@ -188,20 +205,31 @@
 
     a_copies = [{}, {}]
 
-    def a_piece(way, step, ci):
+    def a_piece(way, dist, hops, ci):
         sign = 1 - 2 * way
-        if step > 1:
-            a_copies[way][(step - 1, ci)].wait_recv()
-        ref = ab.at[(y - sign * (step - 1) + ny) % ny, ci]
-        i = (step - 1) * nc + ci
-        a_copies[way][(step, ci)] = send(ref, ref, a_send.at[way, i], a_recv.at[way, i], at_y(sign))
-
-    for step in range(1, hy + 1):
+        ref = ab.at[(y - sign * (dist - hops) + ny) % ny, ci]
+        i = (dist - 1) * nc + ci
+        a_copies[way][(dist, ci)] = send(
+            ref, ref, a_send.at[way, i], a_recv.at[way, i], at_y(sign * hops)
+        )
+
+    def a_all(dist, hops):
         for ci in range(nc):
             for way in (0, 1):
-                if step < hy or ci % 2 == way:
-                    a_piece(way, step, ci)
-        p_both()
+                if dist < hy or ci % 2 == way:
+                    if dist > 2:
+                        a_copies[way][(2, ci)].wait_recv()
+                    a_piece(way, dist, hops, ci)
+
+    if hy > 1:
+        a_all(2, 2)
+    a_all(1, 1)
+    p_both(AFTER_AG1)
+    if hy > 2:
+        a_all(3, 1)
+        for ci in range(nc):
+            a_piece(ci % 2, 4, 2, ci)
+    p_both(AFTER_AG2)
 
     for dx in range(1, nx):
         g_wait[dx - 1].wait_recv()
@@ -211,11 +239,9 @@
         )
 
     for way in (0, 1):
-        for ci in range(nc):
-            if (hy, ci) in a_copies[way]:
-                a_copies[way][(hy, ci)].wait_recv()
-            if hy > 1 and not (hy, ci) in a_copies[way]:
-                a_copies[way][(hy - 1, ci)].wait_recv()
+        for dist, ci in a_copies[way]:
+            if not (dist == 2 and hy > 2):
+                a_copies[way][(dist, ci)].wait_recv()
     for ci in range(nc):
         at[:, ci * toks : (ci + 1) * toks] = ab[:, ci].reshape(toks, feats).T
     for copy in twin_wait:
@@ -248,46 +274,115 @@
         dw_store(slice(k * 256, (k + 1) * 256), total)
     dw_store(slice(mains, mains + 64 * nx), jnp.dot(at[...], rest[...], preferred_element_type=f32))
 
-    z_orders = ring_pieces(hz, 2)
+    zsub = zrows // Z_GROUPS
     z_copies = [{}, {}]
-    half_rows = zrows // 2
-
-    def z_total(way, step, grp, dest):
-        z_copies[way][(step, grp)].wait_recv()
-        sub = slice(grp * half_rows, (grp + 1) * half_rows)
-        return rz[way, step - 1, sub, :].astype(f32)
-
-    def z_piece(way, i):
-        step, grp = z_orders[way][i]
-        sign = 1 - 2 * way
-        dest = (z + sign * (hz + 1 - step) + nz) % nz
-        sub = slice(grp * half_rows, (grp + 1) * half_rows)
-        if (step - 1, grp) in z_copies[way]:
-            total = z_total(way, step - 1, grp, dest) + dwf[dest, sub, :]
-            rz[way, step - 2, sub, :] = total.astype(bf16)
-            src = rz.at[way, step - 2, sub, :]
-        else:
-            src = dwb.at[dest, sub, :]
-        z_copies[way][(step, grp)] = send(
-            src, rz.at[way, step - 1, sub, :], z_send.at[way, i], z_recv.at[way, i], at_z(sign)
-        )
-
-    for i in range(len(z_orders[0])):
-        z_piece(0, i)
-        z_piece(1, i)
-        p_both()
+    halves = [tuple(range(Z_GROUPS // 2)), tuple(range(Z_GROUPS // 2, Z_GROUPS))]
+
+    def z_rows(grp):
+        return slice(grp * zsub, (grp + 1) * zsub)
+
+    def z_got(way, slot, grp):
+        z_copies[way][(slot, grp)].wait_recv()
+        return rz[way, slot, z_rows(grp), :].astype(f32)
+
+    def z_send_piece(way, slot, grp, src, hops):
+        i = slot * Z_GROUPS + grp
+        z_copies[way][(slot, grp)] = send(
+            src, rz.at[way, slot, z_rows(grp), :], z_send.at[way, i], z_recv.at[way, i],
+            at_z((1 - 2 * way) * hops),
+        )
+
+    def z_round(way, slot, off, grp, arrived):
+        dest = (z + (1 - 2 * way) * off + nz) % nz
+        if not arrived:
+            z_send_piece(way, slot, grp, dwb.at[dest, z_rows(grp), :], 1)
+            return
+        total = dwf[dest, z_rows(grp), :]
+        for old in arrived:
+            total = total + z_got(way, old, grp)
+        rz[way, arrived[0], z_rows(grp), :] = total.astype(bf16)
+        z_send_piece(way, slot, grp, rz.at[way, arrived[0], z_rows(grp), :], 1)
+
+    def z_each(slot, off, has):
+        for k in range(Z_GROUPS):
+            for way in (0, 1):
+                order = halves[1 - way] + halves[way]
+                grp = order[k]
+                z_round(way, slot, off, grp, has(way, grp))
+
+    if hz == 4:
+        for k in range(Z_GROUPS // 2):
+            for way in (0, 1):
+                grp = halves[way][k]
+                dest = (z + (1 - 2 * way) * 4 + nz) % nz
+                z_send_piece(way, 0, grp, dwb.at[dest, z_rows(grp), :], 2)
+        z_each(1, 3, lambda way, grp: ())
+    else:
+        for grp in range(Z_GROUPS):
+            way = 0 if grp in halves[0] else 1
+            z_round(way, 0, hz, grp, ())
+
+    for copy in w_wait:
+        copy.wait_recv()
+    weights = jnp.concatenate(
+        [wr[xi, :128, :] for xi in range(nx)] + [wr[xi, 128:, :] for xi in range(nx)], axis=0
+    )
+    for ci in range(nc):
+        both = jnp.concatenate(
+            [ga[ci, xi, :toks, :] for xi in range(nx)] + [rest[ci * toks : (ci + 1) * toks, :]], axis=1
+        )
+        part = jnp.dot(both, weights, preferred_element_type=f32)
+        qp[:, ci] = part.astype(bf16).reshape(ny, per, 128)
+    q_wait = []
+    for near in range(ny // 2, 0, -1):
+        for d in sorted({near, ny - near}):
+            q_wait.append(
+                send(
+                    qp.at[(y + d) % ny], rq.at[d - 1], q_send.at[d - 1], q_recv.at[d - 1], at_y(d)
+                )
+            )
+    p_both(AFTER_Z1)
+
+    if hz == 4:
+        z_each(2, 2, lambda way, grp: (1, 0) if grp in halves[way] else (1,))
+        p_both(AFTER_Z2)
+        z_each(3, 1, lambda way, grp: (2,))
+    else:
+        for step in range(2, hz + 1):
+            z_each(
+                step - 1, hz + 1 - step,
+                lambda way, grp: (step - 2,) if step > 2 or grp in halves[way] else (),
+            )
+    p_both(len(p_orders[0]))
+
+    for copy in q_wait:
+        copy.wait_recv()
+    for ci in range(nc):
+        total = qp[y, ci].astype(f32)
+        for d in range(1, ny):
+            total = total + rq[d - 1, ci].astype(f32)
+        for xi in range(nx):
+            qs[xi * nc + ci] = total[xi * rows : (xi + 1) * rows].astype(bf16)
+    qr[xl * nc + c] = qs[xl * nc + c]
+    o_wait = []
+    for k, (dx, dc) in enumerate(mates):
+        o_wait.append(
+            send(
+                qs.at[(xl + dx) % nx * nc + (c + dc) % nc], qr.at[xl * nc + c],
+                o_send.at[k], o_recv.at[k], at_x(dx, dc),
+            )
+        )
 
     f_wait = []
     sums = []
-    for grp in range(2):
-        sub = slice(grp * half_rows, (grp + 1) * half_rows)
-        total = dwf[z, sub, :]
+    for grp in range(Z_GROUPS):
+        total = dwf[z, z_rows(grp), :]
         for way in (0, 1):
-            if (hz, grp) in z_copies[way]:
-                total = total + z_total(way, hz, grp, z)
+            if (hz - 1, grp) in z_copies[way]:
+                total = total + z_got(way, hz - 1, grp)
         sums.append(total)
-    frows = zrows // nh
-    total = sums if nh == 2 else [jnp.concatenate(sums, axis=0)]
+    some = Z_GROUPS // nh
+    total = [jnp.concatenate(sums[hi * some : (hi + 1) * some], axis=0) for hi in range(nh)]
     for hi in range(nh):
         for xi in range(nx):
             fs[hi, xi, :, :128] = total[hi][:, xi * 128 : (xi + 1) * 128].astype(bf16)
@@ -302,7 +397,6 @@
             )
         )
 
-    p_both(len(p_orders[0]))
     x_wait = {}
     for grp in p_orders_last(p_orders):
         lanes = slice(grp * glanes, (grp + 1) * glanes)
@@ -324,15 +418,17 @@
     for copy in f_wait:
         copy.wait_recv()
     odd = xl % 2 == 1
+    out_rows = []
     for xi in range(nx):
         total = fr[0, xi].astype(f32)
         for hi in range(1, nh):
             total = total + fr[hi, xi].astype(f32)
-        total = total * scale
-        last = total[:, 128:]
-        last = jnp.where(odd, pltpu.roll(last, 64, 1), last)
-        gw_ref[xi * frows : (xi + 1) * frows, :128] = total[:, :128]
-        gw_ref[xi * frows : (xi + 1) * frows, 128:] = last[:, :64]
+        out_rows.append(total * scale)
+    total = jnp.concatenate(out_rows, axis=0)
+    last = total[:, 128:]
+    last = jnp.where(odd, pltpu.roll(last, 64, 1), last)
+    gw_ref[:128, :] = total[:, :128].T
+    gw_ref[128:, :] = last.T[:64]
 
     for grp in p_orders_last(p_orders):
         lanes = slice(grp * glanes, (grp + 1) * glanes)
@@ -342,6 +438,11 @@
             total = total + xr[dx - 1, :, lanes].astype(f32)
         gi_ref[:, lanes] = total.astype(bf16)
 
+    for copy in o_wait:
+        copy.wait_recv()
+    for k in range(nx * nc):
+        gi_ref[:, plain + k * 128 : plain + (k + 1) * 128] = qr[k]
+
     for copy in sent:
         copy.wait_send()
 
@@ -352,10 +453,14 @@
 
 
 def body(dims, act_codes, scale_exps, weight, grad_out):
+    weight, grad_out = weight.T, grad_out.T
+    act_codes, scale_exps, weight, grad_out = (
+        pltpu.with_memory_space_constraint(a, pltpu.HBM) for a in (act_codes, scale_exps, weight, grad_out)
+    )
     nz, nh, nc, nx, ny = dims["z"], dims["xh"], dims["core"], dims["xl"], dims["y"]
     hy, hz = ny // 2, nz // 2
     rows, width = act_codes.shape
-    toks, cols = grad_out.shape
+    cols, toks = grad_out.shape
     out_rows = width // (nz * nh * nc)
     feats = width // (nc * nx)
     per = rows * nx
@@ -363,7 +468,8 @@
     scale = float(1.0 / (toks * nz * nh * nc) ** 0.5)
     bf16, f32 = jnp.bfloat16, jnp.float32
     n_p = GROUPS // 2 + (hy - 1) * GROUPS
-    n_z = 1 + (hz - 1) * 2
+    n_z = hz * Z_GROUPS
+    plain = width - 128 * nc * nx
 
     def vm(shape, kind=bf16):
         return pltpu.VMEM(shape, kind)
@@ -372,15 +478,16 @@
         return pltpu.SemaphoreType.DMA(shape)
 
     scratch = [
-        vm(act_codes.shape), vm(scale_exps.shape, jnp.int32), vm(weight.shape), vm(grad_out.shape),
-        sems(4),
+        vm(act_codes.shape), vm(scale_exps.shape, jnp.int32), vm((cols, plain)),
+        vm((nx - 1, cols, 128)), vm((nx, cols, 128)), vm(grad_out.shape), sems(4 + nx),
         vm((nx * nc, rows, feats)), vm((nx * nc, rows, feats)), vm((ny, nc, per, feats)),
         vm((feats, nc * toks)), vm((toks, cols)), vm((nc, nx, toks * 3 // 2, 128)),
-        vm((nc * toks, 64 * nx)), vm((ny, per, width)), vm((2, hy, per, width)),
-        vm((nx, rows, width)), vm((nx - 1, rows, width)), vm((nx, rows, width), f32),
+        vm((nc * toks, 64 * nx)), vm((ny, per, plain)), vm((2, hy, per, plain)),
+        vm((nx, rows, plain)), vm((nx - 1, rows, plain)), vm((nx, rows, plain), f32),
         vm((nz, feats // nz, dcols), f32), vm((nz, feats // nz, dcols)),
         vm((2, hz, feats // nz, dcols)),
         vm((nh, nx, out_rows // nx, 256)), vm((nh, nx, out_rows // nx, 256)),
+        vm((ny, nc, per, 128)), vm((ny - 1, nc, per, 128)), vm((nx * nc, rows, 128)), vm((nx * nc, rows, 128)),
         sems(nx * nc - 1), sems(nx * nc - 1),
         sems(2, hy * nc), sems(2, hy * nc),
         sems(2 * nx - 1), sems(2 * nx - 1),
@@ -388,21 +495,23 @@
         sems(2, n_z), sems(2, n_z),
         sems(GROUPS, nx - 1), sems(GROUPS, nx - 1),
         sems(nh * nx - 1), sems(nh * nx - 1),
+        sems(nx - 1), sems(nx - 1), sems(ny - 1), sems(ny - 1), sems(nx * nc - 1), sems(nx * nc - 1),
     ]
-    return pl.pallas_call(
+    grad_input, grad_weight = pl.pallas_call(
         functools.partial(kernel, dims, scale),
         out_shape=(
             jax.ShapeDtypeStruct((rows, width), bf16),
-            jax.ShapeDtypeStruct((out_rows, cols), f32),
+            jax.ShapeDtypeStruct((cols, out_rows), f32),
         ),
-        in_specs=[pl.BlockSpec(memory_space=pl.ANY)] * 4,
+        in_specs=[pl.BlockSpec(memory_space=pltpu.HBM)] * 4,
         out_specs=[pl.BlockSpec(memory_space=pltpu.VMEM)] * 2,
         scratch_shapes=scratch,
         compiler_params=pltpu.CompilerParams(
-            collective_id=0, has_side_effects=True, vmem_limit_bytes=48 * 1024 * 1024
+            collective_id=0, has_side_effects=True, vmem_limit_bytes=40 * 1024 * 1024
         ),
         name="backward",
     )(act_codes, scale_exps, weight, grad_out)
+    return grad_input, grad_weight.T
 
 
 def solution(mesh):

time: 70.8 us -> 65.7 us (0.928)
  the two profiles are of different devices: /device:TPU:14 before, /device:TPU:16 now
where the time goes in v2:
time: 65.7 us; the launch traced here: 65.5 us
  Pallas kernels  63.6 us (97%)
  local copies, waits for them, and re-layouts  1.27 us (2%)
    pallas_call x1, Pallas kernels, body(): pl.pallas_call(functools.partial(kernel, dims, scale), out_shape=(jax.Sha...  63.6 us

profile of v2, /device:TPU:16, one launch (start us, length us, event | category | flops | bytes accessed | tf_op | source)
XLA Modules:
  0.0 65.5 jit_solution(4771037692373270345)
XLA Ops:
  0.6 63.6 %backward.1 = (bf16[8,4096]{1,0:T(8,128)(2,1)S(1)}, f32[192,128]{1,0:T(8,128)S(1)}) custom-call(bf16[8,4096]{1,0:T(8,128)(2,1)} %codes_hbm.1, s32[8,32]{1,0:T(8,128)} %exps_hbm.1, bf16[192,4096]{1,0:T(8,128)(2,1)} %bitcast.4, bf16[192,256]{1,0:T(8,128)(2,1)} %bitcast.5), custom_call_target="tpu_custom_call" | custom-call | tf_op jit(solution)/shard_map/backward/pallas_call | solution.py:500
  64.3 0.6 copy.8
  64.9 0.6 copy.9

commit v3 on v2

--- a/solution.py
+++ b/solution.py
@@ -8,9 +8,10 @@
 from jax.sharding import PartitionSpec as P
 
 DIMS = {"z": 8, "xh": 2, "core": 2, "xl": 4, "y": 8}
-GROUPS = 6
+GROUPS = 4
 Z_GROUPS = 4
-AFTER_AG1, AFTER_AG2, AFTER_Z1, AFTER_Z2 = 3, 3, 4, 5
+SHARED = 256
+FIRST, AFTER_AG1, AFTER_AG2, AFTER_Z1, AFTER_Z2 = 6, 0, 4, 2, 2
 
 
 def ring_pieces(half, groups):
@@ -58,7 +59,7 @@
     quarter = 128 // nx
     feats = width // (nc * nx)
     per = rows * nx
-    plain = width - 128 * nc * nx
+    plain = width - SHARED * nc * nx
     glanes = plain // GROUPS
     sent = []
 
@@ -74,8 +75,8 @@
     loads = []
     moves = [(codes_hbm, codes), (exps_hbm, exps), (g_hbm, g), (w_hbm.at[:, :plain], w)]
     for dx in range(nx):
-        first = pl.multiple_of(plain + ((xl + dx) % nx * nc + c) * 128, 128)
-        moves.append((w_hbm.at[:, pl.ds(first, 128)], wq.at[dx - 1] if dx else wr.at[xl]))
+        first = pl.multiple_of(plain + ((xl + dx) % nx * nc + c) * SHARED, SHARED)
+        moves.append((w_hbm.at[:, pl.ds(first, SHARED)], wq.at[dx - 1] if dx else wr.at[xl]))
     for i, (src, dst) in enumerate(moves):
         copy = pltpu.make_async_copy(src, dst, in_sem.at[i])
         copy.start()
@@ -83,7 +84,7 @@
 
     barrier = pltpu.get_barrier_semaphore()
     mates = [(dx, dc) for dx in range(nx) for dc in range(nc) if (dx, dc) != (0, 0)]
-    finals = [(dh, dx) for dh in range(nh) for dx in range(nx) if (dh, dx) != (0, 0)]
+    finals = [(dh, dx) for dh in range(nh)[::-1] for dx in range(nx) if (dh, dx) != (0, 0)]
     peers = [at_x(dx, dc) for dx, dc in mates]
     peers += [at_x(dx, 0, dh) for dh, dx in finals if dh != 0]
     peers += [at_y(d) for d in range(1, ny)]
@@ -194,7 +195,7 @@
             p_piece(0)
             p_piece(1)
 
-    p_both(GROUPS)
+    p_both(FIRST)
 
     for copy in s_wait:
         copy.wait_recv()
@@ -332,7 +333,7 @@
             [ga[ci, xi, :toks, :] for xi in range(nx)] + [rest[ci * toks : (ci + 1) * toks, :]], axis=1
         )
         part = jnp.dot(both, weights, preferred_element_type=f32)
-        qp[:, ci] = part.astype(bf16).reshape(ny, per, 128)
+        qp[:, ci] = part.astype(bf16).reshape(ny, per, SHARED)
     q_wait = []
     for near in range(ny // 2, 0, -1):
         for d in sorted({near, ny - near}):
@@ -385,9 +386,12 @@
     total = [jnp.concatenate(sums[hi * some : (hi + 1) * some], axis=0) for hi in range(nh)]
     for hi in range(nh):
         for xi in range(nx):
-            fs[hi, xi, :, :128] = total[hi][:, xi * 128 : (xi + 1) * 128].astype(bf16)
-            lo = mains + xi // 2 * 128
-            fs[hi, xi, :, 128:] = total[hi][:, lo : lo + 128].astype(bf16)
+            part = total[hi]
+            half = part.shape[0] // 2
+            fs[hi, xi, : 2 * half, :] = part[:, xi * 128 : (xi + 1) * 128].astype(bf16)
+            lo = mains + xi * 64
+            last = part[:, lo : lo + 64]
+            fs[hi, xi, 2 * half :, :] = jnp.concatenate([last[:half], last[half:]], axis=1).astype(bf16)
     fr[xh, xl] = fs[xh, xl]
     for k, (dh, dx) in enumerate(finals):
         f_wait.append(
@@ -417,18 +421,17 @@
 
     for copy in f_wait:
         copy.wait_recv()
-    odd = xl % 2 == 1
-    out_rows = []
+    firsts, lasts = [], []
     for xi in range(nx):
         total = fr[0, xi].astype(f32)
         for hi in range(1, nh):
             total = total + fr[hi, xi].astype(f32)
-        out_rows.append(total * scale)
-    total = jnp.concatenate(out_rows, axis=0)
-    last = total[:, 128:]
-    last = jnp.where(odd, pltpu.roll(last, 64, 1), last)
-    gw_ref[:128, :] = total[:, :128].T
-    gw_ref[128:, :] = last.T[:64]
+        total = total * scale
+        height = total.shape[0] * 2 // 3
+        firsts.append(total[:height])
+        lasts += [total[height:, :64], total[height:, 64:]]
+    gw_ref[:128, :] = jnp.concatenate(firsts, axis=0).T
+    gw_ref[128:, :] = jnp.concatenate(lasts, axis=0).T
 
     for grp in p_orders_last(p_orders):
         lanes = slice(grp * glanes, (grp + 1) * glanes)
@@ -441,7 +444,7 @@
     for copy in o_wait:
         copy.wait_recv()
     for k in range(nx * nc):
-        gi_ref[:, plain + k * 128 : plain + (k + 1) * 128] = qr[k]
+        gi_ref[:, plain + k * SHARED : plain + (k + 1) * SHARED] = qr[k]
 
     for copy in sent:
         copy.wait_send()
@@ -469,7 +472,7 @@
     bf16, f32 = jnp.bfloat16, jnp.float32
     n_p = GROUPS // 2 + (hy - 1) * GROUPS
     n_z = hz * Z_GROUPS
-    plain = width - 128 * nc * nx
+    plain = width - SHARED * nc * nx
 
     def vm(shape, kind=bf16):
         return pltpu.VMEM(shape, kind)
@@ -479,15 +482,16 @@
 
     scratch = [
         vm(act_codes.shape), vm(scale_exps.shape, jnp.int32), vm((cols, plain)),
-        vm((nx - 1, cols, 128)), vm((nx, cols, 128)), vm(grad_out.shape), sems(4 + nx),
+        vm((nx - 1, cols, SHARED)), vm((nx, cols, SHARED)), vm(grad_out.shape), sems(4 + nx),
         vm((nx * nc, rows, feats)), vm((nx * nc, rows, feats)), vm((ny, nc, per, feats)),
         vm((feats, nc * toks)), vm((toks, cols)), vm((nc, nx, toks * 3 // 2, 128)),
         vm((nc * toks, 64 * nx)), vm((ny, per, plain)), vm((2, hy, per, plain)),
         vm((nx, rows, plain)), vm((nx - 1, rows, plain)), vm((nx, rows, plain), f32),
         vm((nz, feats // nz, dcols), f32), vm((nz, feats // nz, dcols)),
         vm((2, hz, feats // nz, dcols)),
-        vm((nh, nx, out_rows // nx, 256)), vm((nh, nx, out_rows // nx, 256)),
-        vm((ny, nc, per, 128)), vm((ny - 1, nc, per, 128)), vm((nx * nc, rows, 128)), vm((nx * nc, rows, 128)),
+        vm((nh, nx, out_rows // nx * 3 // 2, 128)), vm((nh, nx, out_rows // nx * 3 // 2, 128)),
+        vm((ny, nc, per, SHARED)), vm((ny - 1, nc, per, SHARED)),
+        vm((nx * nc, rows, SHARED)), vm((nx * nc, rows, SHARED)),
         sems(nx * nc - 1), sems(nx * nc - 1),
         sems(2, hy * nc), sems(2, hy * nc),
         sems(2 * nx - 1), sems(2 * nx - 1),

time: 65.7 us -> 62.9 us (0.957)
  the two profiles are of different devices: /device:TPU:16 before, /device:TPU:1 now
where the time goes in v3:
time: 62.9 us; the launch traced here: 62.8 us
  Pallas kernels  60.8 us (97%)
  local copies, waits for them, and re-layouts  1.27 us (2%)
  between operations  0.64 us (1%)
    pallas_call x1, Pallas kernels, body(): pl.pallas_call(functools.partial(kernel, dims, scale), out_shape=(jax.Sha...  60.8 us
    unnamed x2, local copies, waits for them, and re-layouts  1.27 us

profile of v3, /device:TPU:1, one launch (start us, length us, event | category | flops | bytes accessed | tf_op | source)
XLA Modules:
  0.0 62.8 jit_solution(4837552920987726672)
XLA Ops:
  0.6 60.8 %backward.1 = (bf16[8,4096]{1,0:T(8,128)(2,1)S(1)}, f32[192,128]{1,0:T(8,128)S(1)}) custom-call(bf16[8,4096]{1,0:T(8,128)(2,1)} %codes_hbm.1, s32[8,32]{1,0:T(8,128)} %exps_hbm.1, bf16[192,4096]{1,0:T(8,128)(2,1)} %bitcast.4, bf16[192,256]{1,0:T(8,128)(2,1)} %bitcast.5), custom_call_target="tpu_custom_call" | custom-call | tf_op jit(solution)/shard_map/backward/pallas_call | solution.py:504
  61.5 0.6 %copy.8 = bf16[8,4096]{1,0:T(8,128)(2,1)} copy(bf16[8,4096]{1,0:T(8,128)(2,1)S(1)} %get-tuple-element.8) | data formatting | bytes 131072
  62.1 0.6 %copy.9 = f32[128,192]{0,1:T(8,128)} copy(f32[128,192]{0,1:T(8,128)S(1)} %bitcast.3) | data formatting | bytes 196608

commit v4 on v3

--- a/solution.py
+++ b/solution.py
@@ -9,7 +9,7 @@
 
 DIMS = {"z": 8, "xh": 2, "core": 2, "xl": 4, "y": 8}
 GROUPS = 4
-Z_GROUPS = 4
+Z_GROUPS = 2
 SHARED = 256
 FIRST, AFTER_AG1, AFTER_AG2, AFTER_Z1, AFTER_Z2 = 6, 0, 4, 2, 2
 
@@ -58,6 +58,7 @@
     blocks = exps.shape[1]
     quarter = 128 // nx
     feats = width // (nc * nx)
+    pfeats = feats // nh
     per = rows * nx
     plain = width - SHARED * nc * nx
     glanes = plain // GROUPS
@@ -101,7 +102,13 @@
     ]
     for xi in range(nx):
         for ci in range(nc):
-            mine = [acts[b] for b in range(blocks) if b % nc == ci]
+            mine = []
+            for part in range(nh):
+                for zi in range(nz):
+                    block = acts[(zi * nh + (part + 1) % nh) * nc + ci]
+                    if nh == 2:
+                        block = jnp.where(xh == 0, block, acts[(zi * nh + part) * nc + ci])
+                    mine.append(block)
             for m in range(len(mine) // nx):
                 out = mine[m * nx]
                 if xi:
@@ -200,36 +207,44 @@
     for copy in s_wait:
         copy.wait_recv()
     for ci in range(nc):
-        ab[y, ci] = jnp.concatenate(
-            [a1[xi * nc + ci].astype(f32) for xi in range(nx)], axis=0
-        ).astype(bf16)
+        block = jnp.concatenate([a1[xi * nc + ci].astype(f32) for xi in range(nx)], axis=0).astype(bf16)
+        for part in range(nh):
+            ab[y, part, ci] = block[:, part * pfeats : (part + 1) * pfeats]
 
     a_copies = [{}, {}]
 
-    def a_piece(way, dist, hops, ci):
+    def a_piece(part, way, dist, hops, ci):
         sign = 1 - 2 * way
-        ref = ab.at[(y - sign * (dist - hops) + ny) % ny, ci]
-        i = (dist - 1) * nc + ci
-        a_copies[way][(dist, ci)] = send(
+        ref = ab.at[(y - sign * (dist - hops) + ny) % ny, part, ci]
+        i = ((dist - 1) * nc + ci) * nh + part
+        a_copies[way][(part, dist, ci)] = send(
             ref, ref, a_send.at[way, i], a_recv.at[way, i], at_y(sign * hops)
         )
 
-    def a_all(dist, hops):
+    def a_all(part, dist, hops):
         for ci in range(nc):
             for way in (0, 1):
                 if dist < hy or ci % 2 == way:
                     if dist > 2:
-                        a_copies[way][(2, ci)].wait_recv()
-                    a_piece(way, dist, hops, ci)
-
-    if hy > 1:
-        a_all(2, 2)
-    a_all(1, 1)
+                        a_copies[way][(part, 2, ci)].wait_recv()
+                    a_piece(part, way, dist, hops, ci)
+
+    def a_wait(part):
+        for way in (0, 1):
+            for one, dist, ci in a_copies[way]:
+                if one == part and not (dist == 2 and hy > 2):
+                    a_copies[way][(one, dist, ci)].wait_recv()
+
+    for part in range(nh):
+        if hy > 1:
+            a_all(part, 2, 2)
+        a_all(part, 1, 1)
     p_both(AFTER_AG1)
     if hy > 2:
-        a_all(3, 1)
-        for ci in range(nc):
-            a_piece(ci % 2, 4, 2, ci)
+        for part in range(nh):
+            a_all(part, 3, 1)
+            for ci in range(nc):
+                a_piece(part, ci % 2, 4, 2, ci)
     p_both(AFTER_AG2)
 
     for dx in range(1, nx):
@@ -239,12 +254,6 @@
             send(ref, ref, g_send.at[nx - 1 + dx], g_recv.at[nx - 1 + dx], at_x(0, 1))
         )
 
-    for way in (0, 1):
-        for dist, ci in a_copies[way]:
-            if not (dist == 2 and hy > 2):
-                a_copies[way][(dist, ci)].wait_recv()
-    for ci in range(nc):
-        at[:, ci * toks : (ci + 1) * toks] = ab[:, ci].reshape(toks, feats).T
     for copy in twin_wait:
         copy.wait_recv()
 
@@ -259,21 +268,26 @@
             lanes = slice(k * 128, (k + 1) * 128)
             rest[ci * toks : ci * toks + toks // 2, lanes] = top.astype(bf16)
             rest[ci * toks + toks // 2 : (ci + 1) * toks, lanes] = bottom.astype(bf16)
-    zrows = feats // nz
-
-    def dw_store(lanes, value):
-        value = value.reshape(nz, zrows, value.shape[1])
-        dwf[:, :, lanes] = value
-        dwb[:, :, lanes] = value.astype(bf16)
-
-    for k in range(nx // 2):
-        total = None
+    zrows = pfeats // nz
+
+    def dw_part(part):
+        feat = slice(part * pfeats, (part + 1) * pfeats)
         for ci in range(nc):
-            both = jnp.concatenate([ga[ci, 2 * k, :toks, :], ga[ci, 2 * k + 1, :toks, :]], axis=1)
-            part = jnp.dot(at[:, ci * toks : (ci + 1) * toks], both, preferred_element_type=f32)
-            total = part if total is None else total + part
-        dw_store(slice(k * 256, (k + 1) * 256), total)
-    dw_store(slice(mains, mains + 64 * nx), jnp.dot(at[...], rest[...], preferred_element_type=f32))
+            at[feat, ci * toks : (ci + 1) * toks] = ab[:, part, ci].reshape(toks, pfeats).T
+
+        def store(lanes, value):
+            value = value.reshape(nz, zrows, value.shape[1])
+            dwf[part, :, :, lanes] = value
+            dwb[part, :, :, lanes] = value.astype(bf16)
+
+        for k in range(nx // 2):
+            total = None
+            for ci in range(nc):
+                both = jnp.concatenate([ga[ci, 2 * k, :toks, :], ga[ci, 2 * k + 1, :toks, :]], axis=1)
+                some = jnp.dot(at[feat, ci * toks : (ci + 1) * toks], both, preferred_element_type=f32)
+                total = some if total is None else total + some
+            store(slice(k * 256, (k + 1) * 256), total)
+        store(slice(mains, mains + 64 * nx), jnp.dot(at[feat, :], rest[...], preferred_element_type=f32))
 
     zsub = zrows // Z_GROUPS
     z_copies = [{}, {}]
@@ -282,46 +296,52 @@
     def z_rows(grp):
         return slice(grp * zsub, (grp + 1) * zsub)
 
-    def z_got(way, slot, grp):
-        z_copies[way][(slot, grp)].wait_recv()
-        return rz[way, slot, z_rows(grp), :].astype(f32)
-
-    def z_send_piece(way, slot, grp, src, hops):
-        i = slot * Z_GROUPS + grp
-        z_copies[way][(slot, grp)] = send(
-            src, rz.at[way, slot, z_rows(grp), :], z_send.at[way, i], z_recv.at[way, i],
+    def z_got(part, way, slot, grp):
+        z_copies[way][(part, slot, grp)].wait_recv()
+        return rz[way, slot, part, z_rows(grp), :].astype(f32)
+
+    def z_send_piece(part, way, slot, grp, src, hops):
+        i = (slot * nh + part) * Z_GROUPS + grp
+        z_copies[way][(part, slot, grp)] = send(
+            src, rz.at[way, slot, part, z_rows(grp), :], z_send.at[way, i], z_recv.at[way, i],
             at_z((1 - 2 * way) * hops),
         )
 
-    def z_round(way, slot, off, grp, arrived):
+    def z_round(part, way, slot, off, grp, arrived):
         dest = (z + (1 - 2 * way) * off + nz) % nz
         if not arrived:
-            z_send_piece(way, slot, grp, dwb.at[dest, z_rows(grp), :], 1)
+            z_send_piece(part, way, slot, grp, dwb.at[part, dest, z_rows(grp), :], 1)
             return
-        total = dwf[dest, z_rows(grp), :]
+        total = dwf[part, dest, z_rows(grp), :]
         for old in arrived:
-            total = total + z_got(way, old, grp)
-        rz[way, arrived[0], z_rows(grp), :] = total.astype(bf16)
-        z_send_piece(way, slot, grp, rz.at[way, arrived[0], z_rows(grp), :], 1)
-
-    def z_each(slot, off, has):
+            total = total + z_got(part, way, old, grp)
+        rz[way, arrived[0], part, z_rows(grp), :] = total.astype(bf16)
+        z_send_piece(part, way, slot, grp, rz.at[way, arrived[0], part, z_rows(grp), :], 1)
+
+    def z_each(part, slot, off, has):
         for k in range(Z_GROUPS):
             for way in (0, 1):
                 order = halves[1 - way] + halves[way]
                 grp = order[k]
-                z_round(way, slot, off, grp, has(way, grp))
-
-    if hz == 4:
-        for k in range(Z_GROUPS // 2):
-            for way in (0, 1):
-                grp = halves[way][k]
-                dest = (z + (1 - 2 * way) * 4 + nz) % nz
-                z_send_piece(way, 0, grp, dwb.at[dest, z_rows(grp), :], 2)
-        z_each(1, 3, lambda way, grp: ())
-    else:
-        for grp in range(Z_GROUPS):
-            way = 0 if grp in halves[0] else 1
-            z_round(way, 0, hz, grp, ())
+                z_round(part, way, slot, off, grp, has(way, grp))
+
+    def z_first(part):
+        if hz == 4:
+            for k in range(Z_GROUPS // 2):
+                for way in (0, 1):
+                    grp = halves[way][k]
+                    dest = (z + (1 - 2 * way) * 4 + nz) % nz
+                    z_send_piece(part, way, 0, grp, dwb.at[part, dest, z_rows(grp), :], 2)
+            z_each(part, 1, 3, lambda way, grp: ())
+        else:
+            for grp in range(Z_GROUPS):
+                way = 0 if grp in halves[0] else 1
+                z_round(part, way, 0, hz, grp, ())
+
+    for part in range(nh):
+        a_wait(part)
+        dw_part(part)
+        z_first(part)
 
     for copy in w_wait:
         copy.wait_recv()
@@ -345,15 +365,18 @@
     p_both(AFTER_Z1)
 
     if hz == 4:
-        z_each(2, 2, lambda way, grp: (1, 0) if grp in halves[way] else (1,))
+        for part in range(nh):
+            z_each(part, 2, 2, lambda way, grp: (1, 0) if grp in halves[way] else (1,))
         p_both(AFTER_Z2)
-        z_each(3, 1, lambda way, grp: (2,))
+        for part in range(nh):
+            z_each(part, 3, 1, lambda way, grp: (2,))
     else:
         for step in range(2, hz + 1):
-            z_each(
-                step - 1, hz + 1 - step,
-                lambda way, grp: (step - 2,) if step > 2 or grp in halves[way] else (),
-            )
+            for part in range(nh):
+                z_each(
+                    part, step - 1, hz + 1 - step,
+                    lambda way, grp: (step - 2,) if step > 2 or grp in halves[way] else (),
+                )
     p_both(len(p_orders[0]))
 
     for copy in q_wait:
@@ -375,31 +398,32 @@
         )
 
     f_wait = []
-    sums = []
-    for grp in range(Z_GROUPS):
-        total = dwf[z, z_rows(grp), :]
-        for way in (0, 1):
-            if (hz - 1, grp) in z_copies[way]:
-                total = total + z_got(way, hz - 1, grp)
-        sums.append(total)
-    some = Z_GROUPS // nh
-    total = [jnp.concatenate(sums[hi * some : (hi + 1) * some], axis=0) for hi in range(nh)]
-    for hi in range(nh):
+    for part in range(nh):
+        sums = []
+        for grp in range(Z_GROUPS):
+            total = dwf[part, z, z_rows(grp), :]
+            for way in (0, 1):
+                if (part, hz - 1, grp) in z_copies[way]:
+                    total = total + z_got(part, way, hz - 1, grp)
+            sums.append(total)
+        total = jnp.concatenate(sums, axis=0)
+        half = zrows // 2
         for xi in range(nx):
-            part = total[hi]
-            half = part.shape[0] // 2
-            fs[hi, xi, : 2 * half, :] = part[:, xi * 128 : (xi + 1) * 128].astype(bf16)
+            fs[part, xi, :zrows, :] = total[:, xi * 128 : (xi + 1) * 128].astype(bf16)
             lo = mains + xi * 64
-            last = part[:, lo : lo + 64]
-            fs[hi, xi, 2 * half :, :] = jnp.concatenate([last[:half], last[half:]], axis=1).astype(bf16)
-    fr[xh, xl] = fs[xh, xl]
-    for k, (dh, dx) in enumerate(finals):
-        f_wait.append(
-            send(
-                fs.at[(xh + dh) % nh, (xl + dx) % nx], fr.at[xh, xl],
-                f_send.at[k], f_recv.at[k], at_x(dx, 0, dh),
-            )
-        )
+            last = total[:, lo : lo + 64]
+            fs[part, xi, zrows:, :] = jnp.concatenate([last[:half], last[half:]], axis=1).astype(bf16)
+        dh = (part + 1) % nh
+        if dh == 0:
+            fr[xh, xl] = fs[part, xl]
+        for k, (far, dx) in enumerate(finals):
+            if far == dh:
+                f_wait.append(
+                    send(
+                        fs.at[part, (xl + dx) % nx], fr.at[xh, xl],
+                        f_send.at[k], f_recv.at[k], at_x(dx, 0, dh),
+                    )
+                )
 
     x_wait = {}
     for grp in p_orders_last(p_orders):
@@ -471,7 +495,7 @@
     scale = float(1.0 / (toks * nz * nh * nc) ** 0.5)
     bf16, f32 = jnp.bfloat16, jnp.float32
     n_p = GROUPS // 2 + (hy - 1) * GROUPS
-    n_z = hz * Z_GROUPS
+    n_z = hz * nh * Z_GROUPS
     plain = width - SHARED * nc * nx
 
     def vm(shape, kind=bf16):
@@ -483,17 +507,17 @@
     scratch = [
         vm(act_codes.shape), vm(scale_exps.shape, jnp.int32), vm((cols, plain)),
         vm((nx - 1, cols, SHARED)), vm((nx, cols, SHARED)), vm(grad_out.shape), sems(4 + nx),
-        vm((nx * nc, rows, feats)), vm((nx * nc, rows, feats)), vm((ny, nc, per, feats)),
+        vm((nx * nc, rows, feats)), vm((nx * nc, rows, feats)), vm((ny, nh, nc, per, feats // nh)),
         vm((feats, nc * toks)), vm((toks, cols)), vm((nc, nx, toks * 3 // 2, 128)),
         vm((nc * toks, 64 * nx)), vm((ny, per, plain)), vm((2, hy, per, plain)),
         vm((nx, rows, plain)), vm((nx - 1, rows, plain)), vm((nx, rows, plain), f32),
-        vm((nz, feats // nz, dcols), f32), vm((nz, feats // nz, dcols)),
-        vm((2, hz, feats // nz, dcols)),
+        vm((nh, nz, feats // nh // nz, dcols), f32), vm((nh, nz, feats // nh // nz, dcols)),
+        vm((2, hz, nh, feats // nh // nz, dcols)),
         vm((nh, nx, out_rows // nx * 3 // 2, 128)), vm((nh, nx, out_rows // nx * 3 // 2, 128)),
         vm((ny, nc, per, SHARED)), vm((ny - 1, nc, per, SHARED)),
         vm((nx * nc, rows, SHARED)), vm((nx * nc, rows, SHARED)),
         sems(nx * nc - 1), sems(nx * nc - 1),
-        sems(2, hy * nc), sems(2, hy * nc),
+        sems(2, hy * nc * nh), sems(2, hy * nc * nh),
         sems(2 * nx - 1), sems(2 * nx - 1),
         sems(2, n_p), sems(2, n_p),
         sems(2, n_z), sems(2, n_z),

time: 62.9 us -> 62.7 us (level)
  no operation moved by 1% of the time
where the time goes in v4:
time: 62.7 us; the launch traced here: 62.5 us
  Pallas kernels  60.6 us (97%)
  local copies, waits for them, and re-layouts  1.27 us (2%)
  between operations  0.64 us (1%)
    pallas_call x1, Pallas kernels, body(): pl.pallas_call(functools.partial(kernel, dims, scale), out_shape=(jax.Sha...  60.6 us
    unnamed x2, local copies, waits for them, and re-layouts  1.27 us

profile of v4, /device:TPU:1, one launch (start us, length us, event | category | flops | bytes accessed | tf_op | source)
XLA Modules:
  0.0 62.5 jit_solution(2810649182356796843)
XLA Ops:
  0.6 60.6 %backward.1 = (bf16[8,4096]{1,0:T(8,128)(2,1)S(1)}, f32[192,128]{1,0:T(8,128)S(1)}) custom-call(bf16[8,4096]{1,0:T(8,128)(2,1)} %codes_hbm.1, s32[8,32]{1,0:T(8,128)} %exps_hbm.1, bf16[192,4096]{1,0:T(8,128)(2,1)} %bitcast.4, bf16[192,256]{1,0:T(8,128)(2,1)} %bitcast.5), custom_call_target="tpu_custom_call" | custom-call | tf_op jit(solution)/shard_map/backward/pallas_call | solution.py:528
  61.2 0.6 %copy.8 = bf16[8,4096]{1,0:T(8,128)(2,1)} copy(bf16[8,4096]{1,0:T(8,128)(2,1)S(1)} %get-tuple-element.8) | data formatting | bytes 131072
  61.9 0.6 %copy.9 = f32[128,192]{0,1:T(8,128)} copy(f32[128,192]{0,1:T(8,128)S(1)} %bitcast.3) | data formatting | bytes 196608

commit v5 on v4

--- a/solution.py
+++ b/solution.py
@@ -1,4 +1,5 @@
 import functools
+import math
 
 import jax
 import jax.numpy as jnp
@@ -26,13 +27,12 @@
 
 
 def kernel(
-    dims, scale, codes_hbm, exps_hbm, w_hbm, g_hbm, gi_ref, gw_ref,
+    dims, scale, codes_hbm, exps_hbm, w_hbm, g_hbm, gi_out, gw_out,
+    gi_ref, gw_ref, out_sem,
     codes, exps, w, wq, wr, g, in_sem,
     s_buf, a1, ab, at, gp, ga, rest, parts, rb, xs, xr, own,
     dwf, dwb, rz, fs, fr, qp, rq, qs, qr,
-    s_send, s_recv, a_send, a_recv, g_send, g_recv, p_send, p_recv,
-    z_send, z_recv, x_send, x_recv, f_send, f_recv,
-    w_send, w_recv, q_send, q_recv, o_send, o_recv,
+    gone, filler, s_recv, a_recv, g_recv, p_recv, z_recv, x_recv, f_recv, w_recv, q_recv, o_recv,
 ):
     nz, nh, nc, nx, ny = dims["z"], dims["xh"], dims["core"], dims["xl"], dims["y"]
     hy, hz = ny // 2, nz // 2
@@ -62,15 +62,15 @@
     per = rows * nx
     plain = width - SHARED * nc * nx
     glanes = plain // GROUPS
-    sent = []
-
-    def send(src, dst, ssem, rsem, dev):
+    sent = {}
+
+    def send(src, dst, kind, rsem, dev):
         copy = pltpu.make_async_remote_copy(
-            src_ref=src, dst_ref=dst, send_sem=ssem, recv_sem=rsem,
+            src_ref=src, dst_ref=dst, send_sem=gone.at[kind], recv_sem=rsem,
             device_id=dev, device_id_type=pl.DeviceIdType.MESH,
         )
         copy.start()
-        sent.append(copy)
+        sent[kind] = sent.get(kind, 0) + math.prod(src.shape)
         return copy
 
     loads = []
@@ -142,16 +142,16 @@
         s_wait.append(
             send(
                 s_buf.at[(xl + dx) % nx * nc + (c + dc) % nc], a1.at[xl * nc + c],
-                s_send.at[k], s_recv.at[k], at_x(dx, dc),
+                0, s_recv.at[k], at_x(dx, dc),
             )
         )
     g_wait = []
     for dx in range(1, nx):
         g_wait.append(
-            send(ga.at[c, xl], ga.at[c, xl], g_send.at[dx - 1], g_recv.at[dx - 1], at_x(dx))
+            send(ga.at[c, xl], ga.at[c, xl], 2, g_recv.at[dx - 1], at_x(dx))
         )
     twin_wait = [
-        send(ga.at[c, xl], ga.at[c, xl], g_send.at[nx - 1], g_recv.at[nx - 1], at_x(0, 1))
+        send(ga.at[c, xl], ga.at[c, xl], 2, g_recv.at[nx - 1], at_x(0, 1))
     ]
 
     w_wait = []
@@ -159,7 +159,7 @@
         loads[4 + dx].wait()
         if dx:
             w_wait.append(
-                send(wq.at[dx - 1], wr.at[xl], w_send.at[dx - 1], w_recv.at[dx - 1], at_x(dx))
+                send(wq.at[dx - 1], wr.at[xl], 7, w_recv.at[dx - 1], at_x(dx))
             )
 
     loads[3].wait()
@@ -194,7 +194,7 @@
             src = parts.at[dest, :, lanes]
         i = p_index[way][(step, grp)]
         p_copies[way][(step, grp)] = send(
-            src, rb.at[way, step - 1, :, lanes], p_send.at[way, i], p_recv.at[way, i], at_y(sign)
+            src, rb.at[way, step - 1, :, lanes], 3, p_recv.at[way, i], at_y(sign)
         )
 
     def p_both(count=1):
@@ -218,7 +218,7 @@
         ref = ab.at[(y - sign * (dist - hops) + ny) % ny, part, ci]
         i = ((dist - 1) * nc + ci) * nh + part
         a_copies[way][(part, dist, ci)] = send(
-            ref, ref, a_send.at[way, i], a_recv.at[way, i], at_y(sign * hops)
+            ref, ref, 1, a_recv.at[way, i], at_y(sign * hops)
         )
 
     def a_all(part, dist, hops):
@@ -251,7 +251,7 @@
         g_wait[dx - 1].wait_recv()
         ref = ga.at[c, (xl - dx + nx) % nx]
         twin_wait.append(
-            send(ref, ref, g_send.at[nx - 1 + dx], g_recv.at[nx - 1 + dx], at_x(0, 1))
+            send(ref, ref, 2, g_recv.at[nx - 1 + dx], at_x(0, 1))
         )
 
     for copy in twin_wait:
@@ -303,7 +303,7 @@
     def z_send_piece(part, way, slot, grp, src, hops):
         i = (slot * nh + part) * Z_GROUPS + grp
         z_copies[way][(part, slot, grp)] = send(
-            src, rz.at[way, slot, part, z_rows(grp), :], z_send.at[way, i], z_recv.at[way, i],
+            src, rz.at[way, slot, part, z_rows(grp), :], 4, z_recv.at[way, i],
             at_z((1 - 2 * way) * hops),
         )
 
@@ -359,7 +359,7 @@
         for d in sorted({near, ny - near}):
             q_wait.append(
                 send(
-                    qp.at[(y + d) % ny], rq.at[d - 1], q_send.at[d - 1], q_recv.at[d - 1], at_y(d)
+                    qp.at[(y + d) % ny], rq.at[d - 1], 8, q_recv.at[d - 1], at_y(d)
                 )
             )
     p_both(AFTER_Z1)
@@ -393,7 +393,7 @@
         o_wait.append(
             send(
                 qs.at[(xl + dx) % nx * nc + (c + dc) % nc], qr.at[xl * nc + c],
-                o_send.at[k], o_recv.at[k], at_x(dx, dc),
+                9, o_recv.at[k], at_x(dx, dc),
             )
         )
 
@@ -421,7 +421,7 @@
                 f_wait.append(
                     send(
                         fs.at[part, (xl + dx) % nx], fr.at[xh, xl],
-                        f_send.at[k], f_recv.at[k], at_x(dx, 0, dh),
+                        6, f_recv.at[k], at_x(dx, 0, dh),
                     )
                 )
 
@@ -440,7 +440,7 @@
         for dx in range(1, nx):
             x_wait[(grp, dx)] = send(
                 xs.at[(xl + dx) % nx, :, lanes], xr.at[dx - 1, :, lanes],
-                x_send.at[grp, dx - 1], x_recv.at[grp, dx - 1], at_x(dx),
+                5, x_recv.at[grp, dx - 1], at_x(dx),
             )
 
     for copy in f_wait:
@@ -456,6 +456,20 @@
         lasts += [total[height:, :64], total[height:, 64:]]
     gw_ref[:128, :] = jnp.concatenate(firsts, axis=0).T
     gw_ref[128:, :] = jnp.concatenate(lasts, axis=0).T
+    outs = [pltpu.make_async_copy(gw_ref, gw_out, out_sem.at[0])]
+    outs[0].start()
+
+    def put(first, size, i):
+        lanes = pl.ds(first, size)
+        copy = pltpu.make_async_copy(gi_ref.at[:, lanes], gi_out.at[:, lanes], out_sem.at[i])
+        copy.start()
+        outs.append(copy)
+
+    for copy in o_wait:
+        copy.wait_recv()
+    for k in range(nx * nc):
+        gi_ref[:, plain + k * SHARED : plain + (k + 1) * SHARED] = qr[k]
+    put(plain, width - plain, 1)
 
     for grp in p_orders_last(p_orders):
         lanes = slice(grp * glanes, (grp + 1) * glanes)
@@ -464,14 +478,13 @@
             x_wait[(grp, dx)].wait_recv()
             total = total + xr[dx - 1, :, lanes].astype(f32)
         gi_ref[:, lanes] = total.astype(bf16)
-
-    for copy in o_wait:
-        copy.wait_recv()
-    for k in range(nx * nc):
-        gi_ref[:, plain + k * SHARED : plain + (k + 1) * SHARED] = qr[k]
-
-    for copy in sent:
-        copy.wait_send()
+        put(grp * glanes, glanes, 2 + grp)
+
+    for kind, size in sent.items():
+        same = filler.at[pl.ds(0, size // 128), :]
+        pltpu.make_async_copy(same, same, gone.at[kind]).wait()
+    for copy in outs:
+        copy.wait()
 
 
 def p_orders_last(orders):
@@ -505,6 +518,7 @@
         return pltpu.SemaphoreType.DMA(shape)
 
     scratch = [
+        vm(act_codes.shape), vm((cols, out_rows), f32), sems(2 + GROUPS),
         vm(act_codes.shape), vm(scale_exps.shape, jnp.int32), vm((cols, plain)),
         vm((nx - 1, cols, SHARED)), vm((nx, cols, SHARED)), vm(grad_out.shape), sems(4 + nx),
         vm((nx * nc, rows, feats)), vm((nx * nc, rows, feats)), vm((ny, nh, nc, per, feats // nh)),
@@ -516,14 +530,8 @@
         vm((nh, nx, out_rows // nx * 3 // 2, 128)), vm((nh, nx, out_rows // nx * 3 // 2, 128)),
         vm((ny, nc, per, SHARED)), vm((ny - 1, nc, per, SHARED)),
         vm((nx * nc, rows, SHARED)), vm((nx * nc, rows, SHARED)),
-        sems(nx * nc - 1), sems(nx * nc - 1),
-        sems(2, hy * nc * nh), sems(2, hy * nc * nh),
-        sems(2 * nx - 1), sems(2 * nx - 1),
-        sems(2, n_p), sems(2, n_p),
-        sems(2, n_z), sems(2, n_z),
-        sems(GROUPS, nx - 1), sems(GROUPS, nx - 1),
-        sems(nh * nx - 1), sems(nh * nx - 1),
-        sems(nx - 1), sems(nx - 1), sems(ny - 1), sems(ny - 1), sems(nx * nc - 1), sems(nx * nc - 1),
+        sems(10), vm((ny * per * width // 128, 128)),
+        sems(nx * nc - 1), sems(2, hy * nc * nh), sems(2 * nx - 1), sems(2, n_p), sems(2, n_z), sems(GROUPS, nx - 1), sems(nh * nx - 1), sems(nx - 1), sems(ny - 1), sems(nx * nc - 1),
     ]
     grad_input, grad_weight = pl.pallas_call(
         functools.partial(kernel, dims, scale),
@@ -532,7 +540,7 @@
             jax.ShapeDtypeStruct((cols, out_rows), f32),
         ),
         in_specs=[pl.BlockSpec(memory_space=pltpu.HBM)] * 4,
-        out_specs=[pl.BlockSpec(memory_space=pltpu.VMEM)] * 2,
+        out_specs=[pl.BlockSpec(memory_space=pl.ANY)] * 2,
         scratch_shapes=scratch,
         compiler_params=pltpu.CompilerParams(
             collective_id=0, has_side_effects=True, vmem_limit_bytes=40 * 1024 * 1024

time: 62.7 us -> 61.4 us (0.979)
  Pallas kernels: 60.6 us -> 59.3 us
    pallas_call x1, Pallas kernels: 60.6 us -> 59.3 us  [body(): pl.pallas_call(functools.partial(kernel, dims, scale), out_shape=(jax.Sha...]
where the time goes in v5:
time: 61.4 us; the launch traced here: 61.2 us
  Pallas kernels  59.3 us (97%)
  local copies, waits for them, and re-layouts  1.27 us (2%)
  between operations  0.64 us (1%)
    pallas_call x1, Pallas kernels, body(): pl.pallas_call(functools.partial(kernel, dims, scale), out_shape=(jax.Sha...  59.3 us
    unnamed x2, local copies, waits for them, and re-layouts  1.27 us

profile of v5, /device:TPU:1, one launch (start us, length us, event | category | flops | bytes accessed | tf_op | source)
XLA Modules:
  0.0 61.2 jit_solution(14719229336726186356)
XLA Ops:
  0.6 59.3 %backward.1 = (bf16[8,4096]{1,0:T(8,128)(2,1)S(1)}, f32[192,128]{1,0:T(8,128)S(1)}) custom-call(bf16[8,4096]{1,0:T(8,128)(2,1)} %codes_hbm.1, s32[8,32]{1,0:T(8,128)} %exps_hbm.1, bf16[192,4096]{1,0:T(8,128)(2,1)} %bitcast.4, bf16[192,256]{1,0:T(8,128)(2,1)} %bitcast.5), custom_call_target="tpu_custom_call" | custom-call | tf_op jit(solution)/shard_map/backward/pallas_call | solution.py:536
  59.9 0.6 %copy.8 = bf16[8,4096]{1,0:T(8,128)(2,1)} copy(bf16[8,4096]{1,0:T(8,128)(2,1)S(1)} %get-tuple-element.8) | data formatting | bytes 131072
  60.6 0.6 %copy.9 = f32[128,192]{0,1:T(8,128)} copy(f32[128,192]{0,1:T(8,128)S(1)} %bitcast.3) | data formatting | bytes 196608

commit v6 on v5

--- a/solution.py
+++ b/solution.py
@@ -72,6 +72,10 @@
         copy.start()
         sent[kind] = sent.get(kind, 0) + math.prod(src.shape)
         return copy
+
+    def wait_all(sem, size):
+        same = filler.at[pl.ds(0, size // 128), :]
+        pltpu.make_async_copy(same, same, sem).wait()
 
     loads = []
     moves = [(codes_hbm, codes), (exps_hbm, exps), (g_hbm, g), (w_hbm.at[:, :plain], w)]
@@ -142,7 +146,7 @@
         s_wait.append(
             send(
                 s_buf.at[(xl + dx) % nx * nc + (c + dc) % nc], a1.at[xl * nc + c],
-                0, s_recv.at[k], at_x(dx, dc),
+                0, s_recv.at[0], at_x(dx, dc),
             )
         )
     g_wait = []
@@ -159,7 +163,7 @@
         loads[4 + dx].wait()
         if dx:
             w_wait.append(
-                send(wq.at[dx - 1], wr.at[xl], 7, w_recv.at[dx - 1], at_x(dx))
+                send(wq.at[dx - 1], wr.at[xl], 7, w_recv.at[0], at_x(dx))
             )
 
     loads[3].wait()
@@ -204,8 +208,7 @@
 
     p_both(FIRST)
 
-    for copy in s_wait:
-        copy.wait_recv()
+    wait_all(s_recv.at[0], len(mates) * rows * feats)
     for ci in range(nc):
         block = jnp.concatenate([a1[xi * nc + ci].astype(f32) for xi in range(nx)], axis=0).astype(bf16)
         for part in range(nh):
@@ -251,11 +254,10 @@
         g_wait[dx - 1].wait_recv()
         ref = ga.at[c, (xl - dx + nx) % nx]
         twin_wait.append(
-            send(ref, ref, 2, g_recv.at[nx - 1 + dx], at_x(0, 1))
-        )
-
-    for copy in twin_wait:
-        copy.wait_recv()
+            send(ref, ref, 2, g_recv.at[nx - 1], at_x(0, 1))
+        )
+
+    wait_all(g_recv.at[nx - 1], nx * (toks * 3 // 2) * 128)
 
     mains = nx * 128
     for ci in range(nc):
@@ -343,8 +345,7 @@
         dw_part(part)
         z_first(part)
 
-    for copy in w_wait:
-        copy.wait_recv()
+    wait_all(w_recv.at[0], (nx - 1) * cols * SHARED)
     weights = jnp.concatenate(
         [wr[xi, :128, :] for xi in range(nx)] + [wr[xi, 128:, :] for xi in range(nx)], axis=0
     )
@@ -359,7 +360,7 @@
         for d in sorted({near, ny - near}):
             q_wait.append(
                 send(
-                    qp.at[(y + d) % ny], rq.at[d - 1], 8, q_recv.at[d - 1], at_y(d)
+                    qp.at[(y + d) % ny], rq.at[d - 1], 8, q_recv.at[0], at_y(d)
                 )
             )
     p_both(AFTER_Z1)
@@ -379,8 +380,7 @@
                 )
     p_both(len(p_orders[0]))
 
-    for copy in q_wait:
-        copy.wait_recv()
+    wait_all(q_recv.at[0], (ny - 1) * nc * per * SHARED)
     for ci in range(nc):
         total = qp[y, ci].astype(f32)
         for d in range(1, ny):
@@ -393,7 +393,7 @@
         o_wait.append(
             send(
                 qs.at[(xl + dx) % nx * nc + (c + dc) % nc], qr.at[xl * nc + c],
-                9, o_recv.at[k], at_x(dx, dc),
+                9, o_recv.at[0], at_x(dx, dc),
             )
         )
 
@@ -421,7 +421,7 @@
                 f_wait.append(
                     send(
                         fs.at[part, (xl + dx) % nx], fr.at[xh, xl],
-                        6, f_recv.at[k], at_x(dx, 0, dh),
+                        6, f_recv.at[0], at_x(dx, 0, dh),
                     )
                 )
 
@@ -440,11 +440,10 @@
         for dx in range(1, nx):
             x_wait[(grp, dx)] = send(
                 xs.at[(xl + dx) % nx, :, lanes], xr.at[dx - 1, :, lanes],
-                5, x_recv.at[grp, dx - 1], at_x(dx),
+                5, x_recv.at[grp], at_x(dx),
             )
 
-    for copy in f_wait:
-        copy.wait_recv()
+    wait_all(f_recv.at[0], len(finals) * math.prod(fr.shape[2:]))
     firsts, lasts = [], []
     for xi in range(nx):
         total = fr[0, xi].astype(f32)
@@ -465,24 +464,22 @@
         copy.start()
         outs.append(copy)
 
-    for copy in o_wait:
-        copy.wait_recv()
+    wait_all(o_recv.at[0], len(mates) * rows * SHARED)
     for k in range(nx * nc):
         gi_ref[:, plain + k * SHARED : plain + (k + 1) * SHARED] = qr[k]
     put(plain, width - plain, 1)
 
     for grp in p_orders_last(p_orders):
         lanes = slice(grp * glanes, (grp + 1) * glanes)
+        wait_all(x_recv.at[grp], (nx - 1) * rows * glanes)
         total = own[xl, :, lanes]
         for dx in range(1, nx):
-            x_wait[(grp, dx)].wait_recv()
             total = total + xr[dx - 1, :, lanes].astype(f32)
         gi_ref[:, lanes] = total.astype(bf16)
         put(grp * glanes, glanes, 2 + grp)
 
     for kind, size in sent.items():
-        same = filler.at[pl.ds(0, size // 128), :]
-        pltpu.make_async_copy(same, same, gone.at[kind]).wait()
+        wait_all(gone.at[kind], size)
     for copy in outs:
         copy.wait()
 
@@ -531,7 +528,7 @@
         vm((ny, nc, per, SHARED)), vm((ny - 1, nc, per, SHARED)),
         vm((nx * nc, rows, SHARED)), vm((nx * nc, rows, SHARED)),
         sems(10), vm((ny * per * width // 128, 128)),
-        sems(nx * nc - 1), sems(2, hy * nc * nh), sems(2 * nx - 1), sems(2, n_p), sems(2, n_z), sems(GROUPS, nx - 1), sems(nh * nx - 1), sems(nx - 1), sems(ny - 1), sems(nx * nc - 1),
+        sems(1), sems(2, hy * nc * nh), sems(nx), sems(2, n_p), sems(2, n_z), sems(GROUPS), sems(1), sems(1), sems(1), sems(1),
     ]
     grad_input, grad_weight = pl.pallas_call(
         functools.partial(kernel, dims, scale),

time: 61.4 us -> 61.1 us (level)
  no operation moved by 1% of the time
where the time goes in v6:
time: 61.1 us; the launch traced here: 60.9 us
  Pallas kernels  59 us (97%)
  local copies, waits for them, and re-layouts  1.27 us (2%)
  between operations  0.64 us (1%)
    pallas_call x1, Pallas kernels, body(): pl.pallas_call(functools.partial(kernel, dims, scale), out_shape=(jax.Sha...  59 us
    unnamed x2, local copies, waits for them, and re-layouts  1.27 us

profile of v6, /device:TPU:1, one launch (start us, length us, event | category | flops | bytes accessed | tf_op | source)
XLA Modules:
  0.0 60.9 jit_solution(1377509814104795070)
XLA Ops:
  0.6 59.0 %backward.1 = (bf16[8,4096]{1,0:T(8,128)(2,1)S(1)}, f32[192,128]{1,0:T(8,128)S(1)}) custom-call(bf16[8,4096]{1,0:T(8,128)(2,1)} %codes_hbm.1, s32[8,32]{1,0:T(8,128)} %exps_hbm.1, bf16[192,4096]{1,0:T(8,128)(2,1)} %bitcast.4, bf16[192,256]{1,0:T(8,128)(2,1)} %bitcast.5), custom_call_target="tpu_custom_call" | custom-call | tf_op jit(solution)/shard_map/backward/pallas_call | solution.py:533
  59.6 0.6 %copy.8 = bf16[8,4096]{1,0:T(8,128)(2,1)} copy(bf16[8,4096]{1,0:T(8,128)(2,1)S(1)} %get-tuple-element.8) | data formatting | bytes 131072
  60.3 0.6 %copy.9 = f32[128,192]{0,1:T(8,128)} copy(f32[128,192]{0,1:T(8,128)S(1)} %bitcast.3) | data formatting | bytes 196608
